TPU v7x, 128 devices: a whole 4x4x4 slice. The times are simulated.
128 devices in a mesh: gx: 128 (over z, y, x, core).
Axes of the slice: x: 4, y: 4, z: 4, core: 2. Of those that a mesh axis runs over, the one named last changes fastest.
Arguments:
- value: float32 [256, 48, 32, 128], P('gx'), may hold values from -6 to 6
- target: float32 [256, 48, 32, 128], P('gx'), may hold values from -6 to 6
- obstacle: float32 [256, 48, 32, 128], P('gx'), may hold values from -6 to -0.5
- fractions: float32 [16, 4], replicated, may hold values from 0 to 1
- control_cost: float32 [16], replicated, may hold values from 0 to 0.5
- shard_offset: int32 [16], replicated, may hold values from -8 to 8, as said below
- cell_offset: int32 [16], replicated, may hold values from 0 to 1
- grid_offset: int32 [16, 3], replicated, may hold values from -4 to 4
Outputs:
- updated: float32 [256, 48, 32, 128], P('gx')
Inputs may be any that keep to these rules, and one draw needn't show every extreme that they name: `shard_offset`: every draw holds both -8 and 8.
All inputs are finite; a program needn't handle non-finite values.
Results may differ from a plain program's by a relative error of at most 0.00002.
Values sent between devices are 32-bit elements; how exact they have to be, the bound alone decides.
No kernel may reach another device: no remote copies, remote signals or barrier semaphores. Data moves between devices by JAX's collectives and lax.ppermute only.
A program may use at most 128 MiB of HBM per device.

v0:
```python
import jax
import jax.numpy as jnp
from jax import lax
from jax.sharding import PartitionSpec as P

NCTRL = 16
REACH = 8


def passed_along(x, axis, by):
    size = lax.axis_size(axis)
    return lax.ppermute(x, axis, [(i, (i + by) % size) for i in range(size)])


def blend(low, high, frac):
    return (1.0 - frac) * low + frac * high


def body(value, target, obstacle, fractions, control_cost, shard_offset, cell_offset, grid_offset):
    rows = value.shape[0]
    count = 2 * REACH + 2
    above = []
    current = value
    for step in range(REACH + 1):
        current = passed_along(current, "gx", -1)
        above.append(current)
    below = []
    current = value
    for step in range(REACH):
        current = passed_along(current, "gx", 1)
        below.append(current)
    pieces = below[::-1] + [value] + above

    def make_branch(offset):

        def branch(start):
            joined = jnp.concatenate([pieces[offset], pieces[offset + 1]], axis=0)
            return lax.dynamic_slice_in_dim(joined, start, rows + 1, 0)

        return branch

    branches = [make_branch(offset) for offset in range(count - 1)]

    def one_control(u, best):
        needed = lax.switch(shard_offset[u] + REACH, branches, cell_offset[u])
        field = blend(needed[:rows], needed[1:], fractions[u, 0])
        for axis_k in range(1, 4):
            moved = grid_offset[u, axis_k - 1]
            field = blend(
                jnp.roll(field, -moved, axis=axis_k),
                jnp.roll(field, -moved - 1, axis=axis_k),
                fractions[u, axis_k],
            )
        return jnp.minimum(best, field + control_cost[u])

    start = jnp.full(value.shape, jnp.inf, jnp.float32)
    best = lax.fori_loop(0, NCTRL, one_control, start)
    return jnp.maximum(obstacle, jnp.minimum(target, best))


def solution(mesh):
    return jax.shard_map(
        body,
        mesh=mesh,
        in_specs=(
            P("gx", None, None, None),
            P("gx", None, None, None),
            P("gx", None, None, None),
            P(),
            P(),
            P(),
            P(),
            P(),
        ),
        out_specs=P("gx", None, None, None),
        check_vma=False,
    )
```

profile of v0, /device:TPU:0, one launch (start us, length us, event | category | flops | bytes accessed | tf_op | source)
XLA Modules:
  0.0 656.6 jit_solution(16560613202821557267)
XLA Ops:
  0.0 8.2 %collective-permute-start.8 = (f32[2,48,32,128]{3,2,1,0:T(8,128)}, f32[2,48,32,128]{3,2,1,0:T(8,128)S(1)}, u32[]{:S(2)}, u32[]{:S(2)}) collective-permute-start(f32[2,48,32,128]{3,2,1,0:T(8,128)} %param.33), channel_id=1, source_target_pairs={{0,127},{1,0},{2,1},{3,2},{4,3},{5,4},{6,5},{7,6},{8,7},{9,8},{10,... | collective-permute-start | bytes 4718600 | tf_op jit(solution)/shard_map/ppermute | solution.py:12
  8.2 18.2 %collective-permute-done.8 = f32[2,48,32,128]{3,2,1,0:T(8,128)S(1)} collective-permute-done((f32[2,48,32,128]{3,2,1,0:T(8,128)}, f32[2,48,32,128]{3,2,1,0:T(8,128)S(1)}, u32[]{:S(2)}, u32[]{:S(2)}) %collective-permute-start.8) | collective-permute-done | bytes 1572896 | tf_op jit(solution)/shard_map/ppermute | solution.py:12
  27.6 7.2 %collective-permute-start.9 = (f32[2,48,32,128]{3,2,1,0:T(8,128)S(1)}, f32[2,48,32,128]{3,2,1,0:T(8,128)S(1)}, u32[]{:S(2)}, u32[]{:S(2)}) collective-permute-start(f32[2,48,32,128]{3,2,1,0:T(8,128)S(1)} %collective-permute-done.8), channel_id=1, source_target_pairs={{0,127},{1,0},{2,1},{3,2},{4,3},{5,4},{6,5},{7,6},{8,7},{9,8},{10,... | collective-permute-start | bytes 4718600 | tf_op jit(solution)/shard_map/ppermute | solution.py:12
  34.9 17.9 %collective-permute-done.9 = f32[2,48,32,128]{3,2,1,0:T(8,128)S(1)} collective-permute-done((f32[2,48,32,128]{3,2,1,0:T(8,128)S(1)}, f32[2,48,32,128]{3,2,1,0:T(8,128)S(1)}, u32[]{:S(2)}, u32[]{:S(2)}) %collective-permute-start.9) | collective-permute-done | bytes 1572896 | tf_op jit(solution)/shard_map/ppermute | solution.py:12
  52.8 7.3 %collective-permute-start.10 = (f32[2,48,32,128]{3,2,1,0:T(8,128)S(1)}, f32[2,48,32,128]{3,2,1,0:T(8,128)S(1)}, u32[]{:S(2)}, u32[]{:S(2)}) collective-permute-start(f32[2,48,32,128]{3,2,1,0:T(8,128)S(1)} %collective-permute-done.9), channel_id=1, source_target_pairs={{0,127},{1,0},{2,1},{3,2},{4,3},{5,4},{6,5},{7,6},{8,7},{9,8},{10,... | collective-permute-start | bytes 4718600 | tf_op jit(solution)/shard_map/ppermute | solution.py:12
  60.2 17.8 %collective-permute-done.10 = f32[2,48,32,128]{3,2,1,0:T(8,128)S(1)} collective-permute-done((f32[2,48,32,128]{3,2,1,0:T(8,128)S(1)}, f32[2,48,32,128]{3,2,1,0:T(8,128)S(1)}, u32[]{:S(2)}, u32[]{:S(2)}) %collective-permute-start.10) | collective-permute-done | bytes 1572896 | tf_op jit(solution)/shard_map/ppermute | solution.py:12
  78.1 7.3 %collective-permute-start.11 = (f32[2,48,32,128]{3,2,1,0:T(8,128)S(1)}, f32[2,48,32,128]{3,2,1,0:T(8,128)S(1)}, u32[]{:S(2)}, u32[]{:S(2)}) collective-permute-start(f32[2,48,32,128]{3,2,1,0:T(8,128)S(1)} %collective-permute-done.10), channel_id=1, source_target_pairs={{0,127},{1,0},{2,1},{3,2},{4,3},{5,4},{6,5},{7,6},{8,7},{9,8},{10,... | collective-permute-start | bytes 4718600 | tf_op jit(solution)/shard_map/ppermute | solution.py:12
  85.5 17.8 %collective-permute-done.11 = f32[2,48,32,128]{3,2,1,0:T(8,128)S(1)} collective-permute-done((f32[2,48,32,128]{3,2,1,0:T(8,128)S(1)}, f32[2,48,32,128]{3,2,1,0:T(8,128)S(1)}, u32[]{:S(2)}, u32[]{:S(2)}) %collective-permute-start.11) | collective-permute-done | bytes 1572896 | tf_op jit(solution)/shard_map/ppermute | solution.py:12
  103.4 7.3 %collective-permute-start.12 = (f32[2,48,32,128]{3,2,1,0:T(8,128)S(1)}, f32[2,48,32,128]{3,2,1,0:T(8,128)S(1)}, u32[]{:S(2)}, u32[]{:S(2)}) collective-permute-start(f32[2,48,32,128]{3,2,1,0:T(8,128)S(1)} %collective-permute-done.11), channel_id=1, source_target_pairs={{0,127},{1,0},{2,1},{3,2},{4,3},{5,4},{6,5},{7,6},{8,7},{9,8},{10,... | collective-permute-start | bytes 4718600 | tf_op jit(solution)/shard_map/ppermute | solution.py:12
  110.8 17.8 %collective-permute-done.12 = f32[2,48,32,128]{3,2,1,0:T(8,128)S(1)} collective-permute-done((f32[2,48,32,128]{3,2,1,0:T(8,128)S(1)}, f32[2,48,32,128]{3,2,1,0:T(8,128)S(1)}, u32[]{:S(2)}, u32[]{:S(2)}) %collective-permute-start.12) | collective-permute-done | bytes 1572896 | tf_op jit(solution)/shard_map/ppermute | solution.py:12
  128.6 7.3 %collective-permute-start.13 = (f32[2,48,32,128]{3,2,1,0:T(8,128)S(1)}, f32[2,48,32,128]{3,2,1,0:T(8,128)S(1)}, u32[]{:S(2)}, u32[]{:S(2)}) collective-permute-start(f32[2,48,32,128]{3,2,1,0:T(8,128)S(1)} %collective-permute-done.12), channel_id=1, source_target_pairs={{0,127},{1,0},{2,1},{3,2},{4,3},{5,4},{6,5},{7,6},{8,7},{9,8},{10,... | collective-permute-start | bytes 4718600 | tf_op jit(solution)/shard_map/ppermute | solution.py:12
  136.1 17.8 %collective-permute-done.13 = f32[2,48,32,128]{3,2,1,0:T(8,128)S(1)} collective-permute-done((f32[2,48,32,128]{3,2,1,0:T(8,128)S(1)}, f32[2,48,32,128]{3,2,1,0:T(8,128)S(1)}, u32[]{:S(2)}, u32[]{:S(2)}) %collective-permute-start.13) | collective-permute-done | bytes 1572896 | tf_op jit(solution)/shard_map/ppermute | solution.py:12
  153.9 7.3 %collective-permute-start.14 = (f32[2,48,32,128]{3,2,1,0:T(8,128)S(1)}, f32[2,48,32,128]{3,2,1,0:T(8,128)S(1)}, u32[]{:S(2)}, u32[]{:S(2)}) collective-permute-start(f32[2,48,32,128]{3,2,1,0:T(8,128)S(1)} %collective-permute-done.13), channel_id=1, source_target_pairs={{0,127},{1,0},{2,1},{3,2},{4,3},{5,4},{6,5},{7,6},{8,7},{9,8},{10,... | collective-permute-start | bytes 4718600 | tf_op jit(solution)/shard_map/ppermute | solution.py:12
  161.3 17.8 %collective-permute-done.14 = f32[2,48,32,128]{3,2,1,0:T(8,128)S(1)} collective-permute-done((f32[2,48,32,128]{3,2,1,0:T(8,128)S(1)}, f32[2,48,32,128]{3,2,1,0:T(8,128)S(1)}, u32[]{:S(2)}, u32[]{:S(2)}) %collective-permute-start.14) | collective-permute-done | bytes 1572896 | tf_op jit(solution)/shard_map/ppermute | solution.py:12
  179.2 7.3 %collective-permute-start.15 = (f32[2,48,32,128]{3,2,1,0:T(8,128)S(1)}, f32[2,48,32,128]{3,2,1,0:T(8,128)S(1)}, u32[]{:S(2)}, u32[]{:S(2)}) collective-permute-start(f32[2,48,32,128]{3,2,1,0:T(8,128)S(1)} %collective-permute-done.14), channel_id=1, source_target_pairs={{0,127},{1,0},{2,1},{3,2},{4,3},{5,4},{6,5},{7,6},{8,7},{9,8},{10,... | collective-permute-start | bytes 4718600 | tf_op jit(solution)/shard_map/ppermute | solution.py:12
  186.7 17.8 %collective-permute-done.15 = f32[2,48,32,128]{3,2,1,0:T(8,128)S(1)} collective-permute-done((f32[2,48,32,128]{3,2,1,0:T(8,128)S(1)}, f32[2,48,32,128]{3,2,1,0:T(8,128)S(1)}, u32[]{:S(2)}, u32[]{:S(2)}) %collective-permute-start.15) | collective-permute-done | bytes 1572896 | tf_op jit(solution)/shard_map/ppermute | solution.py:12
  204.5 7.3 %collective-permute-start.16 = (f32[2,48,32,128]{3,2,1,0:T(8,128)S(1)}, f32[2,48,32,128]{3,2,1,0:T(8,128)}, u32[]{:S(2)}, u32[]{:S(2)}) collective-permute-start(f32[2,48,32,128]{3,2,1,0:T(8,128)S(1)} %collective-permute-done.15), channel_id=1, source_target_pairs={{0,127},{1,0},{2,1},{3,2},{4,3},{5,4},{6,5},{7,6},{8,7},{9,8},{10,... | collective-permute-start | bytes 4718600 | tf_op jit(solution)/shard_map/ppermute | solution.py:12
  212.3 17.4 %collective-permute-done.16 = f32[2,48,32,128]{3,2,1,0:T(8,128)} collective-permute-done((f32[2,48,32,128]{3,2,1,0:T(8,128)S(1)}, f32[2,48,32,128]{3,2,1,0:T(8,128)}, u32[]{:S(2)}, u32[]{:S(2)}) %collective-permute-start.16) | collective-permute-done | bytes 1572896 | tf_op jit(solution)/shard_map/ppermute | solution.py:12
  229.7 422.8 %while.17 = (s32[]{:T(128)}, f32[2,48,32,128]{3,2,1,0:T(8,128)}, f32[16,4]{0,1:T(4,128)}, s32[16]{0:T(128)}, s32[16]{0:T(128)}, /*index=5*/f32[2,48,32,128]{3,2,...) while((s32[]{:T(128)}, f32[2,48,32,128]{3,2,1,0:T(8,128)}, ...), condition=%wide.region_18.22_spmd.clone, body=%wide.region_0.21_spmd.clone.sunk | while | flops 9044067 | bytes 40898644 | solution.py:57
  232.8 3.4 conditional.3
  243.3 3.3 fusion.23
  251.5 4.2 fusion.25
  258.8 2.2 conditional.3
  268.0 3.4 fusion.23
  276.4 5.6 fusion.25
  294.4 3.4 fusion.23
  302.6 5.6 fusion.25
  311.3 2.2 conditional.3
  320.6 3.3 fusion.23
  328.8 5.6 fusion.25
  337.5 3.4 conditional.3
  348.0 3.4 fusion.23
  356.3 5.6 fusion.25
  365.0 3.4 conditional.3
  375.4 3.4 fusion.23
  383.7 5.6 fusion.25
  392.4 2.2 conditional.3
  401.7 3.3 fusion.23
  409.9 5.6 fusion.25
  427.9 3.4 fusion.23
  436.1 5.6 fusion.25
  444.8 2.2 conditional.3
  454.1 3.3 fusion.23
  462.3 5.6 fusion.25
  480.3 3.4 fusion.23
  488.6 5.6 fusion.25
  497.4 3.4 conditional.3
  507.8 3.3 fusion.23
  516.0 5.6 fusion.25
  524.7 2.2 conditional.3
  534.0 3.3 fusion.23
  542.2 5.6 fusion.25
  550.9 2.2 conditional.3
  560.2 3.3 fusion.23
  568.3 5.6 fusion.25
  577.0 2.2 conditional.3
  586.3 3.3 fusion.23
  594.5 5.6 fusion.25
  603.2 2.2 conditional.3
  612.5 3.3 fusion.23
  620.7 5.6 fusion.25
  638.7 3.4 fusion.23
  646.9 5.6 fusion.25
  652.5 4.0 minimum_maximum_fusion
  (343 shorter events, 183.1 us)
Async XLA Ops:
  0.0 26.5 %collective-permute-start.8 = (f32[2,48,32,128]{3,2,1,0:T(8,128)}, f32[2,48,32,128]{3,2,1,0:T(8,128)S(1)}, u32[]{:S(2)}, u32[]{:S(2)}) collective-permute-start(f32[2,48,32,128]{3,2,1,0:T(8,128)} %param.33), channel_id=1, source_target_pairs={{0,127},{1,0},{2,1},{3,2},{4,3},{5,4},{6,5},{7,6},{8,7},{9,8},{10,... | collective-permute-start | bytes 4718600 | tf_op jit(solution)/shard_map/ppermute | solution.py:12
  8.2 26.6 %collective-permute-start = (f32[2,48,32,128]{3,2,1,0:T(8,128)}, f32[2,48,32,128]{3,2,1,0:T(8,128)S(1)}, u32[]{:S(2)}, u32[]{:S(2)}) collective-permute-start(f32[2,48,32,128]{3,2,1,0:T(8,128)} %param.33), channel_id=1, source_target_pairs={{0,1},{1,2},{2,3},{3,4},{4,5},{5,6},{6,7},{7,8},{8,9},{9,10},{10,1... | collective-permute-start | bytes 4718600 | tf_op jit(solution)/shard_map/ppermute | solution.py:12
  27.6 25.2 %collective-permute-start.9 = (f32[2,48,32,128]{3,2,1,0:T(8,128)S(1)}, f32[2,48,32,128]{3,2,1,0:T(8,128)S(1)}, u32[]{:S(2)}, u32[]{:S(2)}) collective-permute-start(f32[2,48,32,128]{3,2,1,0:T(8,128)S(1)} %collective-permute-done.8), channel_id=1, source_target_pairs={{0,127},{1,0},{2,1},{3,2},{4,3},{5,4},{6,5},{7,6},{8,7},{9,8},{10,... | collective-permute-start | bytes 4718600 | tf_op jit(solution)/shard_map/ppermute | solution.py:12
  34.9 17.9 %copy-start.1 = (f32[2,48,32,128]{3,2,1,0:T(8,128)}, f32[2,48,32,128]{3,2,1,0:T(8,128)S(1)}, u32[]{:S(2)}) copy-start(f32[2,48,32,128]{3,2,1,0:T(8,128)S(1)} %collective-permute-done) | copy-start | bytes 4718596
  34.9 25.3 %collective-permute-start.1 = (f32[2,48,32,128]{3,2,1,0:T(8,128)S(1)}, f32[2,48,32,128]{3,2,1,0:T(8,128)S(1)}, u32[]{:S(2)}, u32[]{:S(2)}) collective-permute-start(f32[2,48,32,128]{3,2,1,0:T(8,128)S(1)} %collective-permute-done), channel_id=1, source_target_pairs={{0,1},{1,2},{2,3},{3,4},{4,5},{5,6},{6,7},{7,8},{8,9},{9,10},{10,1... | collective-permute-start | bytes 4718600 | tf_op jit(solution)/shard_map/ppermute | solution.py:12
  52.8 7.3 %copy-start.2 = (f32[2,48,32,128]{3,2,1,0:T(8,128)}, f32[2,48,32,128]{3,2,1,0:T(8,128)S(1)}, u32[]{:S(2)}) copy-start(f32[2,48,32,128]{3,2,1,0:T(8,128)S(1)} %collective-permute-done.9) | copy-start | bytes 4718596
  52.8 25.3 %collective-permute-start.10 = (f32[2,48,32,128]{3,2,1,0:T(8,128)S(1)}, f32[2,48,32,128]{3,2,1,0:T(8,128)S(1)}, u32[]{:S(2)}, u32[]{:S(2)}) collective-permute-start(f32[2,48,32,128]{3,2,1,0:T(8,128)S(1)} %collective-permute-done.9), channel_id=1, source_target_pairs={{0,127},{1,0},{2,1},{3,2},{4,3},{5,4},{6,5},{7,6},{8,7},{9,8},{10,... | collective-permute-start | bytes 4718600 | tf_op jit(solution)/shard_map/ppermute | solution.py:12
  60.1 17.9 %copy-start.3 = (f32[2,48,32,128]{3,2,1,0:T(8,128)}, f32[2,48,32,128]{3,2,1,0:T(8,128)S(1)}, u32[]{:S(2)}) copy-start(f32[2,48,32,128]{3,2,1,0:T(8,128)S(1)} %collective-permute-done.1) | copy-start | bytes 4718596
  60.1 25.3 %collective-permute-start.2 = (f32[2,48,32,128]{3,2,1,0:T(8,128)S(1)}, f32[2,48,32,128]{3,2,1,0:T(8,128)S(1)}, u32[]{:S(2)}, u32[]{:S(2)}) collective-permute-start(f32[2,48,32,128]{3,2,1,0:T(8,128)S(1)} %collective-permute-done.1), channel_id=1, source_target_pairs={{0,1},{1,2},{2,3},{3,4},{4,5},{5,6},{6,7},{7,8},{8,9},{9,10},{10,1... | collective-permute-start | bytes 4718600 | tf_op jit(solution)/shard_map/ppermute | solution.py:12
  78.1 7.4 %copy-start.4 = (f32[2,48,32,128]{3,2,1,0:T(8,128)}, f32[2,48,32,128]{3,2,1,0:T(8,128)S(1)}, u32[]{:S(2)}) copy-start(f32[2,48,32,128]{3,2,1,0:T(8,128)S(1)} %collective-permute-done.10) | copy-start | bytes 4718596
  78.1 25.3 %collective-permute-start.11 = (f32[2,48,32,128]{3,2,1,0:T(8,128)S(1)}, f32[2,48,32,128]{3,2,1,0:T(8,128)S(1)}, u32[]{:S(2)}, u32[]{:S(2)}) collective-permute-start(f32[2,48,32,128]{3,2,1,0:T(8,128)S(1)} %collective-permute-done.10), channel_id=1, source_target_pairs={{0,127},{1,0},{2,1},{3,2},{4,3},{5,4},{6,5},{7,6},{8,7},{9,8},{10,... | collective-permute-start | bytes 4718600 | tf_op jit(solution)/shard_map/ppermute | solution.py:12
  85.5 17.9 %copy-start.5 = (f32[2,48,32,128]{3,2,1,0:T(8,128)}, f32[2,48,32,128]{3,2,1,0:T(8,128)S(1)}, u32[]{:S(2)}) copy-start(f32[2,48,32,128]{3,2,1,0:T(8,128)S(1)} %collective-permute-done.2) | copy-start | bytes 4718596
  85.5 25.3 %collective-permute-start.3 = (f32[2,48,32,128]{3,2,1,0:T(8,128)S(1)}, f32[2,48,32,128]{3,2,1,0:T(8,128)S(1)}, u32[]{:S(2)}, u32[]{:S(2)}) collective-permute-start(f32[2,48,32,128]{3,2,1,0:T(8,128)S(1)} %collective-permute-done.2), channel_id=1, source_target_pairs={{0,1},{1,2},{2,3},{3,4},{4,5},{5,6},{6,7},{7,8},{8,9},{9,10},{10,1... | collective-permute-start | bytes 4718600 | tf_op jit(solution)/shard_map/ppermute | solution.py:12
  103.4 7.4 %copy-start.6 = (f32[2,48,32,128]{3,2,1,0:T(8,128)}, f32[2,48,32,128]{3,2,1,0:T(8,128)S(1)}, u32[]{:S(2)}) copy-start(f32[2,48,32,128]{3,2,1,0:T(8,128)S(1)} %collective-permute-done.11) | copy-start | bytes 4718596
  103.4 25.3 %collective-permute-start.12 = (f32[2,48,32,128]{3,2,1,0:T(8,128)S(1)}, f32[2,48,32,128]{3,2,1,0:T(8,128)S(1)}, u32[]{:S(2)}, u32[]{:S(2)}) collective-permute-start(f32[2,48,32,128]{3,2,1,0:T(8,128)S(1)} %collective-permute-done.11), channel_id=1, source_target_pairs={{0,127},{1,0},{2,1},{3,2},{4,3},{5,4},{6,5},{7,6},{8,7},{9,8},{10,... | collective-permute-start | bytes 4718600 | tf_op jit(solution)/shard_map/ppermute | solution.py:12
  110.8 17.9 %copy-start.7 = (f32[2,48,32,128]{3,2,1,0:T(8,128)}, f32[2,48,32,128]{3,2,1,0:T(8,128)S(1)}, u32[]{:S(2)}) copy-start(f32[2,48,32,128]{3,2,1,0:T(8,128)S(1)} %collective-permute-done.3) | copy-start | bytes 4718596
  110.8 25.3 %collective-permute-start.4 = (f32[2,48,32,128]{3,2,1,0:T(8,128)S(1)}, f32[2,48,32,128]{3,2,1,0:T(8,128)S(1)}, u32[]{:S(2)}, u32[]{:S(2)}) collective-permute-start(f32[2,48,32,128]{3,2,1,0:T(8,128)S(1)} %collective-permute-done.3), channel_id=1, source_target_pairs={{0,1},{1,2},{2,3},{3,4},{4,5},{5,6},{6,7},{7,8},{8,9},{9,10},{10,1... | collective-permute-start | bytes 4718600 | tf_op jit(solution)/shard_map/ppermute | solution.py:12
  128.6 7.4 %copy-start.8 = (f32[2,48,32,128]{3,2,1,0:T(8,128)}, f32[2,48,32,128]{3,2,1,0:T(8,128)S(1)}, u32[]{:S(2)}) copy-start(f32[2,48,32,128]{3,2,1,0:T(8,128)S(1)} %collective-permute-done.12) | copy-start | bytes 4718596
  128.6 25.3 %collective-permute-start.13 = (f32[2,48,32,128]{3,2,1,0:T(8,128)S(1)}, f32[2,48,32,128]{3,2,1,0:T(8,128)S(1)}, u32[]{:S(2)}, u32[]{:S(2)}) collective-permute-start(f32[2,48,32,128]{3,2,1,0:T(8,128)S(1)} %collective-permute-done.12), channel_id=1, source_target_pairs={{0,127},{1,0},{2,1},{3,2},{4,3},{5,4},{6,5},{7,6},{8,7},{9,8},{10,... | collective-permute-start | bytes 4718600 | tf_op jit(solution)/shard_map/ppermute | solution.py:12
  136.0 17.9 %copy-start.9 = (f32[2,48,32,128]{3,2,1,0:T(8,128)}, f32[2,48,32,128]{3,2,1,0:T(8,128)S(1)}, u32[]{:S(2)}) copy-start(f32[2,48,32,128]{3,2,1,0:T(8,128)S(1)} %collective-permute-done.4) | copy-start | bytes 4718596
  136.0 25.3 %collective-permute-start.5 = (f32[2,48,32,128]{3,2,1,0:T(8,128)S(1)}, f32[2,48,32,128]{3,2,1,0:T(8,128)S(1)}, u32[]{:S(2)}, u32[]{:S(2)}) collective-permute-start(f32[2,48,32,128]{3,2,1,0:T(8,128)S(1)} %collective-permute-done.4), channel_id=1, source_target_pairs={{0,1},{1,2},{2,3},{3,4},{4,5},{5,6},{6,7},{7,8},{8,9},{9,10},{10,1... | collective-permute-start | bytes 4718600 | tf_op jit(solution)/shard_map/ppermute | solution.py:12
  153.9 7.4 %copy-start.10 = (f32[2,48,32,128]{3,2,1,0:T(8,128)}, f32[2,48,32,128]{3,2,1,0:T(8,128)S(1)}, u32[]{:S(2)}) copy-start(f32[2,48,32,128]{3,2,1,0:T(8,128)S(1)} %collective-permute-done.13) | copy-start | bytes 4718596
  153.9 25.3 %collective-permute-start.14 = (f32[2,48,32,128]{3,2,1,0:T(8,128)S(1)}, f32[2,48,32,128]{3,2,1,0:T(8,128)S(1)}, u32[]{:S(2)}, u32[]{:S(2)}) collective-permute-start(f32[2,48,32,128]{3,2,1,0:T(8,128)S(1)} %collective-permute-done.13), channel_id=1, source_target_pairs={{0,127},{1,0},{2,1},{3,2},{4,3},{5,4},{6,5},{7,6},{8,7},{9,8},{10,... | collective-permute-start | bytes 4718600 | tf_op jit(solution)/shard_map/ppermute | solution.py:12
  161.3 17.9 %copy-start.11 = (f32[2,48,32,128]{3,2,1,0:T(8,128)}, f32[2,48,32,128]{3,2,1,0:T(8,128)S(1)}, u32[]{:S(2)}) copy-start(f32[2,48,32,128]{3,2,1,0:T(8,128)S(1)} %collective-permute-done.5) | copy-start | bytes 4718596
  161.3 25.4 %collective-permute-start.6 = (f32[2,48,32,128]{3,2,1,0:T(8,128)S(1)}, f32[2,48,32,128]{3,2,1,0:T(8,128)}, u32[]{:S(2)}, u32[]{:S(2)}) collective-permute-start(f32[2,48,32,128]{3,2,1,0:T(8,128)S(1)} %collective-permute-done.5), channel_id=1, source_target_pairs={{0,1},{1,2},{2,3},{3,4},{4,5},{5,6},{6,7},{7,8},{8,9},{9,10},{10,1... | collective-permute-start | bytes 4718600 | tf_op jit(solution)/shard_map/ppermute | solution.py:12
  179.2 7.5 %copy-start.12 = (f32[2,48,32,128]{3,2,1,0:T(8,128)}, f32[2,48,32,128]{3,2,1,0:T(8,128)S(1)}, u32[]{:S(2)}) copy-start(f32[2,48,32,128]{3,2,1,0:T(8,128)S(1)} %collective-permute-done.14) | copy-start | bytes 4718596
  179.2 25.3 %collective-permute-start.15 = (f32[2,48,32,128]{3,2,1,0:T(8,128)S(1)}, f32[2,48,32,128]{3,2,1,0:T(8,128)S(1)}, u32[]{:S(2)}, u32[]{:S(2)}) collective-permute-start(f32[2,48,32,128]{3,2,1,0:T(8,128)S(1)} %collective-permute-done.14), channel_id=1, source_target_pairs={{0,127},{1,0},{2,1},{3,2},{4,3},{5,4},{6,5},{7,6},{8,7},{9,8},{10,... | collective-permute-start | bytes 4718600 | tf_op jit(solution)/shard_map/ppermute | solution.py:12
  186.7 25.6 %collective-permute-start.7 = (f32[2,48,32,128]{3,2,1,0:T(8,128)}, f32[2,48,32,128]{3,2,1,0:T(8,128)}, u32[]{:S(2)}, u32[]{:S(2)}) collective-permute-start(f32[2,48,32,128]{3,2,1,0:T(8,128)} %collective-permute-done.6), channel_id=1, source_target_pairs={{0,1},{1,2},{2,3},{3,4},{4,5},{5,6},{6,7},{7,8},{8,9},{9,10},{10,1... | collective-permute-start | bytes 4718600 | tf_op jit(solution)/shard_map/ppermute | solution.py:12
  204.5 25.3 %collective-permute-start.16 = (f32[2,48,32,128]{3,2,1,0:T(8,128)S(1)}, f32[2,48,32,128]{3,2,1,0:T(8,128)}, u32[]{:S(2)}, u32[]{:S(2)}) collective-permute-start(f32[2,48,32,128]{3,2,1,0:T(8,128)S(1)} %collective-permute-done.15), channel_id=1, source_target_pairs={{0,127},{1,0},{2,1},{3,2},{4,3},{5,4},{6,5},{7,6},{8,7},{9,8},{10,... | collective-permute-start | bytes 4718600 | tf_op jit(solution)/shard_map/ppermute | solution.py:12
  232.8 5.1 copy-start.17
  251.4 4.2 copy-start.14
  255.7 3.1 copy-start.13
  258.7 3.9 copy-start.17
  276.4 5.6 copy-start.14
  285.0 3.9 copy-start.17
  302.6 5.6 copy-start.14
  308.2 3.1 copy-start.13
  311.3 3.9 copy-start.17
  328.8 5.6 copy-start.14
  337.5 5.1 copy-start.17
  356.3 5.6 copy-start.14
  365.0 5.1 copy-start.17
  383.7 5.6 copy-start.14
  389.3 3.1 copy-start.13
  392.4 3.9 copy-start.17
  409.9 5.6 copy-start.14
  418.6 3.9 copy-start.17
  436.1 5.6 copy-start.14
  444.8 3.9 copy-start.17
  462.3 5.6 copy-start.14
  471.0 3.9 copy-start.17
  488.6 5.6 copy-start.14
  497.3 5.1 copy-start.17
  516.0 5.6 copy-start.14
  524.7 3.9 copy-start.17
  542.2 5.6 copy-start.14
  550.9 3.9 copy-start.17
  568.3 5.6 copy-start.14
  577.0 3.9 copy-start.17
  594.5 5.6 copy-start.14
  603.2 3.9 copy-start.17
  620.7 5.6 copy-start.14
  629.4 3.9 copy-start.17
  646.9 5.6 copy-start.14
  (50 other events, 127.5 us)
where the time goes:
time: 660 us; the launch traced here: 657 us
  other arithmetic  242 us (37%)
  waiting for transfers between devices  162 us (25%)
  loops' own time  109 us (17%)
  local copies, waits for them, and re-layouts  76.6 us (12%)
  starting transfers between devices  66.9 us (10%)
    ppermute x17, waiting for transfers between devices, passed_along(): return lax.ppermute(x, axis, [(i, (i + by) % size) for i in range(size)])  162 us
    add x48, other arithmetic, blend(): return (1.0 - frac) * low + frac * high  115 us
    another operation x1, loops' own time, body(): best = lax.fori_loop(0, NCTRL, one_control, start)  109 us
    min x16, other arithmetic, one_control(): return jnp.minimum(best, field + control_cost[u])  88.3 us
    ppermute x17, starting transfers between devices, passed_along(): return lax.ppermute(x, axis, [(i, (i + by) % size) for i in range(size)])  66.9 us
    dynamic_slice x32, local copies, waits for them, and re-layouts, one_control(): needed = lax.switch(shard_offset[u] + REACH, branches, cell_offset[u])  39.2 us
    concatenate x16, other arithmetic, branch(): joined = jnp.concatenate([pieces[offset], pieces[offset + 1]], axis=0)  35 us
  transfers between devices with their start and end apart: 17, of which 15 were waited for; matrix products, arithmetic and copies ran while one was open for 0% of the time, Pallas kernels for 0%

commit v1 on v0

v1 whole, which is shorter than its diff:
```python
import functools

import jax
import jax.numpy as jnp
import numpy as np
from jax import lax
from jax.experimental import pallas as pl
from jax.experimental.pallas import tpu as pltpu
from jax.sharding import PartitionSpec as P

NCTRL = 16
ROW = 8
NX4 = 4
UNROLL = 16

HBM = pltpu.MemorySpace.HBM
SMEM = pltpu.MemorySpace.SMEM

OWN, SIB, PA, PB, XA, XB, Q, XQ, HA, HXA, HB, HXB = range(12)
N_EARLY = 6


def source_table():
    table = np.zeros((ROW, 9), np.int32)
    for i in range(ROW):
        x, c = i // 2, i % 2
        first = -1 if x % 2 == 0 else 0
        for q in range(9):
            s = first + q
            if s < 0 or s >= ROW:
                if x in (1, 2):
                    direct = 0 if x == 1 else 1
                    table[i, q] = HA if c == direct else HXA
                else:
                    direct = 0 if x == 3 else 1
                    table[i, q] = HB if c == direct else HXB
                continue
            other = (s % 2) != c
            delta = (s // 2 - x) % NX4
            if delta == 0:
                table[i, q] = SIB if other else OWN
            elif delta == 2:
                table[i, q] = XQ if other else Q
            elif (delta == 1) == (c == 0):
                table[i, q] = XA if other else PB
                if delta == 3:
                    table[i, q] = XA if other else PB
            else:
                table[i, q] = XB if other else PA
    return table


def pairs(count, rule):
    out = []
    for d in range(count):
        r, i = divmod(d, ROW)
        to = rule(r, i // 2, i % 2)
        if to is None:
            continue
        r2, x2, c2 = to
        out.append((d, (r2 % (count // ROW)) * ROW + (x2 % NX4) * 2 + c2))
    return out


def blend(low, high, keep, frac):
    return keep * low + frac * high


def control_kernel(mode, nsrc, *refs):
    meta, so, co, goff, frac, cost = refs[:6]
    src = refs[6:6 + nsrc]
    refs = refs[6 + nsrc:]
    nbest = 1 if mode == "rest" else 2
    ninit = {"early": 0, "late": 2, "rest": 1}[mode]
    init, refs = refs[:ninit], refs[ninit:]
    outs, refs = refs[:nbest], refs[nbest:]
    buf, best, todo, sem, io_sem = refs
    ny, nz = best.shape[2], best.shape[3]

    inits = [pltpu.make_async_copy(init[b], best.at[b], io_sem.at[b]) for b in range(ninit)]
    for copy in inits:
        copy.start()

    i, first = meta[0], meta[1]

    def place(u):
        at = i + so[u] - first
        a = jnp.where(at < 0, -1, jnp.where(at >= ROW, 1, 0))
        return a, at - a * ROW

    def listed(u, n):
        a, q = place(u)
        early = jnp.logical_and(meta[2 + q] < N_EARLY, meta[3 + q] < N_EARLY)
        if mode == "rest":
            take = a == 0
        elif mode == "early":
            take = jnp.logical_and(a != 0, early)
        else:
            take = jnp.logical_and(a != 0, jnp.logical_not(early))

        @pl.when(take)
        def _():
            todo[n] = u

        return n + take.astype(jnp.int32)

    count = lax.fori_loop(0, NCTRL, listed, jnp.int32(0))

    def row_copies(ref, half, slot, t):
        return (
            pltpu.make_async_copy(ref.at[half], buf.at[slot, t, :, pl.ds(0, nz), :], sem.at[slot]),
            pltpu.make_async_copy(
                ref.at[half, :, pl.ds(0, 8), :], buf.at[slot, t, :, pl.ds(nz, 8), :], sem.at[slot]
            ),
        )

    def fetch(k):
        u = todo[k]
        slot = lax.rem(k, 2)
        _, q = place(u)

        @pl.loop(0, 3)
        def _(t):
            at = co[u] + t
            half = jnp.bitwise_and(at, 1)
            which = meta[2 + q + jnp.right_shift(at, 1)]
            for n in range(nsrc):

                @pl.when(which == n)
                def _(n=n):
                    for copy in row_copies(src[n], half, slot, t):
                        copy.start()

    def compute(k):
        u = todo[k]
        slot = lax.rem(k, 2)
        a, _ = place(u)
        b = 0 if mode == "rest" else jnp.where(a > 0, 0, 1)
        f = [frac[4 * u + d] for d in range(4)]
        g = [1.0 - x for x in f]
        g1, g2, g3 = (goff[3 * u + d] for d in range(3))
        pay = cost[u]
        low, high = [], []
        for v in range(nz // 8):
            s = 8 * v + g2
            low.append(jnp.where(s < 0, s + nz, s))
            high.append(jnp.where(s + 1 < 0, s + 1 + nz, s + 1))
        turn0 = lax.rem(128 - g3, 128)
        turn1 = lax.rem(127 - g3, 128)

        def plane(y):
            y = jnp.where(y < 0, y + ny, y)
            y = jnp.where(y >= ny, y - ny, y)
            out = [[], []]
            for v in range(nz // 8):
                z = [
                    blend(buf[slot, t, y, pl.ds(low[v], 8), :], buf[slot, t, y, pl.ds(high[v], 8), :], g[2], f[2])
                    for t in range(3)
                ]
                out[0].append(blend(z[0], z[1], g[0], f[0]))
                out[1].append(blend(z[1], z[2], g[0], f[0]))
            return out[0] + out[1]

        def step(m, here):
            for n in range(UNROLL):
                y = m * UNROLL + n
                there = plane(y + g1 + 1)
                for row in range(2):
                    for v in range(nz // 8):
                        w = row * (nz // 8) + v
                        mid = blend(here[w], there[w], g[1], f[1])
                        full = blend(pltpu.roll(mid, turn0, 1), pltpu.roll(mid, turn1, 1), g[3], f[3])
                        at = (b, row, y, pl.ds(8 * v, 8), slice(None))
                        best[at] = jnp.minimum(best[at], full + pay)
                here = there
            return here

        lax.fori_loop(0, ny // UNROLL, step, plane(g1))

    @pl.when(count > 0)
    def _():
        fetch(jnp.int32(0))

    if not ninit:

        @pl.loop(0, ny)
        def _(y):
            for b in range(nbest):
                for row in range(2):
                    best[b, row, y] = jnp.full(best.shape[3:], jnp.inf, jnp.float32)

    for copy in inits:
        copy.wait()

    @pl.loop(0, count)
    def _(k):
        @pl.when(k + 1 < count)
        def _():
            fetch(k + 1)

        @pl.loop(0, 3)
        def _(t):
            for copy in row_copies(src[0], 0, lax.rem(k, 2), t):
                copy.wait()

        compute(k)

    ends = [pltpu.make_async_copy(best.at[b], outs[b], io_sem.at[b]) for b in range(nbest)]
    for copy in ends:
        copy.start()
    for copy in ends:
        copy.wait()


def run_controls(mode, params, sources, init, flops):
    shape = sources[0].shape
    nbest = 1 if mode == "rest" else 2
    out = jax.ShapeDtypeStruct(shape, jnp.float32)
    return pl.pallas_call(
        functools.partial(control_kernel, mode, len(sources)),
        out_shape=[out] * nbest,
        in_specs=[pl.BlockSpec(memory_space=SMEM)] * len(params)
        + [pl.BlockSpec(memory_space=HBM)] * (len(sources) + len(init)),
        out_specs=[pl.BlockSpec(memory_space=HBM)] * nbest,
        scratch_shapes=[
            pltpu.VMEM((2, 3, shape[1], shape[2] + 8, shape[3]), jnp.float32),
            pltpu.VMEM((nbest,) + shape, jnp.float32),
            pltpu.SMEM((NCTRL,), jnp.int32),
            pltpu.SemaphoreType.DMA((2,)),
            pltpu.SemaphoreType.DMA((2,)),
        ],
        compiler_params=pltpu.CompilerParams(vmem_limit_bytes=24 * 2**20),
        cost_estimate=pl.CostEstimate(flops=flops, bytes_accessed=2**20, transcendentals=0),
        name="controls_" + mode,
    )(*params, *sources, *init)


def body(value, target, obstacle, fractions, control_cost, shard_offset, cell_offset, grid_offset):
    size = lax.axis_size("gx")

    def move(x, rule):
        return lax.ppermute(x, "gx", pairs(size, rule))

    swap = lambda r, x, c: (r, x, 1 - c)
    chips = lambda members, rule: lambda r, x, c: rule(r, x, c) if x in members else None

    pa = move(value, lambda r, x, c: (r, x + 1 - 2 * c, c))
    pb = move(value, lambda r, x, c: (r, x - 1 + 2 * c, c))
    sib = move(value, swap)
    q = move(pa, lambda r, x, c: (r, x + 1 - 2 * c, c))
    xa = move(pa, swap)
    xb = move(pb, swap)
    halo = lambda up, down: lambda r, x, c: (
        (r - 1, x, c) if (x, c) == up else (r + 1, x, c) if (x, c) == down else None
    )
    ha = move(pa, halo((1, 0), (2, 1)))
    hb = move(pb, halo((3, 0), (0, 1)))
    hxa = move(ha, lambda r, x, c: (r, x, 1 - c) if (x, c) in ((1, 0), (2, 1)) else None)
    hxb = move(hb, lambda r, x, c: (r, x, 1 - c) if (x, c) in ((3, 0), (0, 1)) else None)
    xq = move(q, swap)

    i = lax.rem(lax.axis_index("gx"), ROW)
    table = source_table()
    first = np.array([-1 if (k // 2) % 2 == 0 else 0 for k in range(ROW)], np.int32)
    meta = jnp.asarray(np.concatenate([np.arange(ROW, dtype=np.int32)[:, None], first[:, None], table], 1))
    meta = lax.dynamic_index_in_dim(meta, i, 0, keepdims=False)
    params = (
        meta,
        shard_offset,
        cell_offset,
        grid_offset.reshape(-1),
        fractions.reshape(-1),
        control_cost,
    )
    early = [value, sib, pa, pb, xa, xb]
    full = early + [q, xq, ha, hxa, hb, hxb]
    up, down = run_controls("early", params, early, [], 2 * 10**7)
    up, down = run_controls("late", params, full, [up, down], 10**7)
    got_up = move(up, lambda r, x, c: (r - 1, x, c))
    got_down = move(down, lambda r, x, c: (r + 1, x, c))
    (mine,) = run_controls("rest", params, full, [target], 3 * 10**7)
    return jnp.maximum(obstacle, jnp.minimum(mine, jnp.minimum(got_up, got_down)))


def solution(mesh):
    return jax.shard_map(
        body,
        mesh=mesh,
        in_specs=(
            P("gx", None, None, None),
            P("gx", None, None, None),
            P("gx", None, None, None),
            P(),
            P(),
            P(),
            P(),
            P(),
        ),
        out_specs=P("gx", None, None, None),
        check_vma=False,
    )
```

time: 660 us -> 140 us (0.21)
  the two profiles are of different devices: /device:TPU:0 before, /device:TPU:2 now
where the time goes in v1:
time: 140 us
  waiting for transfers between devices  76.2 us (54%)
  Pallas kernels  30.1 us (22%)
  starting transfers between devices  23.8 us (17%)
  local copies, waits for them, and re-layouts  8.32 us (6%)
  other arithmetic  1.9 us (1%)
    ppermute x13, waiting for transfers between devices, move(): return lax.ppermute(x, 'gx', pairs(size, rule))  76.2 us
    pallas_call x3, Pallas kernels, run_controls(): pl.pallas_call(functools.partial(control_kernel, mode, len(sources)), out...  30.1 us
    ppermute x13, starting transfers between devices, move(): return lax.ppermute(x, 'gx', pairs(size, rule))  23.8 us
    unnamed x18, local copies, waits for them, and re-layouts  7.45 us
  transfers between devices with their start and end apart: 13, of which 5 were waited for; matrix products, arithmetic and copies ran while one was open for 2% of the time, Pallas kernels for 17%

profile of v1, /device:TPU:2, one launch (start us, length us, event | category | flops | bytes accessed | tf_op | source)
XLA Modules:
  0.0 140.4 jit_solution(2330404258427010847)
XLA Ops:
  0.0 1.5 %collective-permute-start.1 = (f32[2,48,32,128]{3,2,1,0:T(8,128)}, f32[2,48,32,128]{3,2,1,0:T(8,128)S(1)}, u32[]{:S(2)}, u32[]{:S(2)}) collective-permute-start(f32[2,48,32,128]{3,2,1,0:T(8,128)} %refs_6_.5), channel_id=1, source_target_pairs={{0,2},{1,7},{2,4},{3,1},{4,6},{5,3},{6,0},{7,5},{8,10},{9,15},{10,... | collective-permute-start | bytes 4718600 | tf_op jit(solution)/shard_map/ppermute | solution.py:242
  1.5 0.5 collective-permute-start.2
  2.0 0.0 collective-permute-start
  2.0 35.3 %collective-permute-done.1.refs_8_ = f32[2,48,32,128]{3,2,1,0:T(8,128)S(1)} collective-permute-done((f32[2,48,32,128]{3,2,1,0:T(8,128)}, f32[2,48,32,128]{3,2,1,0:T(8,128)S(1)}, u32[]{:S(2)}, u32[]{:S(2)}) %collective-permute-start.1) | collective-permute-done | bytes 1572896 | tf_op jit(solution)/shard_map/ppermute | solution.py:242
  37.3 0.8 collective-permute-start.5
  38.1 8.4 %collective-permute-start.7 = (f32[2,48,32,128]{3,2,1,0:T(8,128)S(1)}, f32[2,48,32,128]{3,2,1,0:T(8,128)}, u32[]{:S(2)}, u32[]{:S(2)}) collective-permute-start(f32[2,48,32,128]{3,2,1,0:T(8,128)S(1)} %collective-permute-done.1.refs_8_), channel_id=1, source_target_pairs={{2,122},{5,13},{10,2},{13,21},{18,10},{21,29},{26,18},{29,37},{34,... | collective-permute-start | bytes 4718600 | tf_op jit(solution)/shard_map/ppermute | solution.py:242
  46.5 0.0 collective-permute-done.2.refs_9_
  46.5 1.8 %collective-permute-start.9 = (f32[2,48,32,128]{3,2,1,0:T(8,128)S(1)}, f32[2,48,32,128]{3,2,1,0:T(8,128)}, u32[]{:S(2)}, u32[]{:S(2)}) collective-permute-start(f32[2,48,32,128]{3,2,1,0:T(8,128)S(1)} %collective-permute-done.2.refs_9_), channel_id=1, source_target_pairs={{1,9},{6,126},{9,17},{14,6},{17,25},{22,14},{25,33},{30,22},{33,41... | collective-permute-start | bytes 4718600 | tf_op jit(solution)/shard_map/ppermute | solution.py:242
  48.3 0.0 collective-permute-start.3
  48.3 0.0 collective-permute-done.refs_7_
  48.3 0.0 copy-start.1
  48.3 1.1 copy-done.1
  49.5 0.5 collective-permute-start.4
  50.0 7.9 %collective-permute-done.5.refs_12_ = f32[2,48,32,128]{3,2,1,0:T(8,128)} collective-permute-done((f32[2,48,32,128]{3,2,1,0:T(8,128)S(1)}, f32[2,48,32,128]{3,2,1,0:T(8,128)}, u32[]{:S(2)}, u32[]{:S(2)}) %collective-permute-start.5) | collective-permute-done | bytes 1572896 | tf_op jit(solution)/shard_map/ppermute | solution.py:242
  57.8 0.0 collective-permute-start.6
  57.8 6.6 %collective-permute-done.7.refs_14_ = f32[2,48,32,128]{3,2,1,0:T(8,128)} collective-permute-done((f32[2,48,32,128]{3,2,1,0:T(8,128)S(1)}, f32[2,48,32,128]{3,2,1,0:T(8,128)}, u32[]{:S(2)}, u32[]{:S(2)}) %collective-permute-start.7) | collective-permute-done | bytes 1572896 | tf_op jit(solution)/shard_map/ppermute | solution.py:242
  64.4 2.5 %collective-permute-start.8 = (f32[2,48,32,128]{3,2,1,0:T(8,128)}, f32[2,48,32,128]{3,2,1,0:T(8,128)}, u32[]{:S(2)}, u32[]{:S(2)}) collective-permute-start(f32[2,48,32,128]{3,2,1,0:T(8,128)} %collective-permute-done.7.refs_14_), channel_id=1, source_target_pairs={{2,3},{5,4},{10,11},{13,12},{18,19},{21,20},{26,27},{29,28},{34,35... | collective-permute-start | bytes 4718600 | tf_op jit(solution)/shard_map/ppermute | solution.py:242
  66.9 0.0 collective-permute-done.9.refs_16_
  66.9 1.8 %collective-permute-start.10 = (f32[2,48,32,128]{3,2,1,0:T(8,128)}, f32[2,48,32,128]{3,2,1,0:T(8,128)}, u32[]{:S(2)}, u32[]{:S(2)}) collective-permute-start(f32[2,48,32,128]{3,2,1,0:T(8,128)} %collective-permute-done.9.refs_16_), channel_id=1, source_target_pairs={{1,0},{6,7},{9,8},{14,15},{17,16},{22,23},{25,24},{30,31},{33,32},... | collective-permute-start | bytes 4718600 | tf_op jit(solution)/shard_map/ppermute | solution.py:242
  68.8 0.8 copy.12
  69.5 0.1 reshape.6.refs_3_
  69.6 0.8 copy.13
  70.4 0.1 reshape.7.refs_4_
  70.5 0.7 dynamic-slice_bitcast_fusion.refs_0_
  71.2 0.0 collective-permute-done.3.refs_10_
  71.2 0.0 collective-permute-done.4.refs_11_
  71.2 0.0 copy-start
  71.2 1.4 copy-done
  72.6 0.0 copy-start.2
  72.6 1.4 %copy-done.2 = f32[2,48,32,128]{3,2,1,0:T(8,128)S(1)} copy-done((f32[2,48,32,128]{3,2,1,0:T(8,128)S(1)}, f32[2,48,32,128]{3,2,1,0:T(8,128)}, u32[]{:S(2)}) %copy-start.2) | copy-done | bytes 1572888
  74.0 0.0 copy-start.4
  74.0 0.7 copy-done.4
  74.6 0.0 copy-start.5
  74.6 0.7 copy-done.5
  75.3 0.0 copy-start.6
  75.3 0.7 copy-done.6
  76.0 14.8 %controls_early.1 = (f32[2,48,32,128]{3,2,1,0:T(8,128)S(1)}, f32[2,48,32,128]{3,2,1,0:T(8,128)S(1)}) custom-call(s32[11]{0:T(128)S(1)} %dynamic-slice_bitcast_fusion.refs_0_, s32[16]{0:T(128)S(1)} %copy-done.4, s32[16]{0:T(128)S(1)} %copy-done.5, s32[48]{0:T(128)S(1)} %reshape.6.refs_3_, f32[64]{0:T(128)S(1)} %reshape.7.refs_4_, f32[16]{0:T(128)S(1)} %copy-done.6, ...), custom_call_target="tpu_custom_call" | custom-call | flops 20000000 | bytes 1048576 | tf_op jit(solution)/shard_map/controls_early/pallas_call | solution.py:219
  90.8 0.0 collective-permute-done.6.refs_13_
  90.8 0.0 collective-permute-done.8.refs_15_
  90.8 0.0 collective-permute-done.10.refs_17_
  90.8 0.0 copy-start.3
  90.8 5.6 %controls_late.1 = (f32[2,48,32,128]{3,2,1,0:T(8,128)S(1)}, f32[2,48,32,128]{3,2,1,0:T(8,128)S(1)}) custom-call(s32[11]{0:T(128)S(1)} %dynamic-slice_bitcast_fusion.refs_0_, s32[16]{0:T(128)S(1)} %copy-done.4, s32[16]{0:T(128)S(1)} %copy-done.5, s32[48]{0:T(128)S(1)} %reshape.6.refs_3_, f32[64]{0:T(128)S(1)} %reshape.7.refs_4_, f32[16]{0:T(128)S(1)} %copy-done.6, ...), custom_call_target="tpu_custom_call" | custom-call | flops 10000000 | bytes 1048576 | tf_op jit(solution)/shard_map/controls_late/pallas_call | solution.py:219
  96.5 6.0 %collective-permute-start.11 = (f32[2,48,32,128]{3,2,1,0:T(8,128)S(1)}, f32[2,48,32,128]{3,2,1,0:T(8,128)S(1)}, u32[]{:S(2)}, u32[]{:S(2)}) collective-permute-start(f32[2,48,32,128]{3,2,1,0:T(8,128)S(1)} %get-tuple-element.11), channel_id=1, source_target_pairs={{0,120},{1,121},{2,122},{3,123},{4,124},{5,125},{6,126},{7,127},{8... | collective-permute-start | bytes 4718600 | tf_op jit(solution)/shard_map/ppermute | solution.py:242
  102.4 0.0 copy-start.7
  102.4 0.0 collective-permute-start.12
  102.4 0.0 copy-done.3
  102.4 9.6 %controls_rest.1 = f32[2,48,32,128]{3,2,1,0:T(8,128)S(1)} custom-call(s32[11]{0:T(128)S(1)} %dynamic-slice_bitcast_fusion.refs_0_, s32[16]{0:T(128)S(1)} %copy-done.4, s32[16]{0:T(128)S(1)} %copy-done.5, s32[48]{0:T(128)S(1)} %reshape.6.refs_3_, f32[64]{0:T(128)S(1)} %reshape.7.refs_4_, f32[16]{0:T(128)S(1)} %copy-done.6, f32[2,48,32,128]{3,2,1,0:T(8,128)S(1)} %copy-done, ...), custom_call_target="tpu_custom_call" | custom-call | flops 30000000 | bytes 1048576 | tf_op jit(solution)/shard_map/controls_rest/pallas_call | solution.py:219
  112.1 20.9 %collective-permute-done.11 = f32[2,48,32,128]{3,2,1,0:T(8,128)S(1)} collective-permute-done((f32[2,48,32,128]{3,2,1,0:T(8,128)S(1)}, f32[2,48,32,128]{3,2,1,0:T(8,128)S(1)}, u32[]{:S(2)}, u32[]{:S(2)}) %collective-permute-start.11) | collective-permute-done | bytes 1572896 | tf_op jit(solution)/shard_map/ppermute | solution.py:242
  133.0 5.5 %collective-permute-done.12 = f32[2,48,32,128]{3,2,1,0:T(8,128)S(1)} collective-permute-done((f32[2,48,32,128]{3,2,1,0:T(8,128)S(1)}, f32[2,48,32,128]{3,2,1,0:T(8,128)S(1)}, u32[]{:S(2)}, u32[]{:S(2)}) %collective-permute-start.12) | collective-permute-done | bytes 1572896 | tf_op jit(solution)/shard_map/ppermute | solution.py:242
  138.5 0.0 copy-done.7
  138.5 1.9 %minimum_maximum_fusion = f32[2,48,32,128]{3,2,1,0:T(8,128)} fusion(f32[2,48,32,128]{3,2,1,0:T(8,128)S(1)} %copy-done.7, f32[2,48,32,128]{3,2,1,0:T(8,128)S(1)} %controls_rest.1, f32[2,48,32,128]{3,2,1,0:T(8,128)S(1)} %collective-permute-done.11, f32[2,48,32,128]{3,2,1,0:T(8,128)S(1)} %collective-permute-done.12), kind=kLoop, calls=%fused_computation | loop fusion | flops 1179648 | bytes 7864320 | tf_op jit(solution)/shard_map/max | solution.py:282
Async XLA Ops:
  0.0 37.3 %collective-permute-start.1 = (f32[2,48,32,128]{3,2,1,0:T(8,128)}, f32[2,48,32,128]{3,2,1,0:T(8,128)S(1)}, u32[]{:S(2)}, u32[]{:S(2)}) collective-permute-start(f32[2,48,32,128]{3,2,1,0:T(8,128)} %refs_6_.5), channel_id=1, source_target_pairs={{0,2},{1,7},{2,4},{3,1},{4,6},{5,3},{6,0},{7,5},{8,10},{9,15},{10,... | collective-permute-start | bytes 4718600 | tf_op jit(solution)/shard_map/ppermute | solution.py:242
  1.5 45.0 %collective-permute-start.2 = (f32[2,48,32,128]{3,2,1,0:T(8,128)}, f32[2,48,32,128]{3,2,1,0:T(8,128)S(1)}, u32[]{:S(2)}, u32[]{:S(2)}) collective-permute-start(f32[2,48,32,128]{3,2,1,0:T(8,128)} %refs_6_.5), channel_id=1, source_target_pairs={{0,6},{1,3},{2,0},{3,5},{4,2},{5,7},{6,4},{7,1},{8,14},{9,11},{10,... | collective-permute-start | bytes 4718600 | tf_op jit(solution)/shard_map/ppermute | solution.py:242
  2.0 46.3 %collective-permute-start = (f32[2,48,32,128]{3,2,1,0:T(8,128)}, f32[2,48,32,128]{3,2,1,0:T(8,128)S(1)}, u32[]{:S(2)}, u32[]{:S(2)}) collective-permute-start(f32[2,48,32,128]{3,2,1,0:T(8,128)} %refs_6_.5), channel_id=1, source_target_pairs={{0,1},{1,0},{2,3},{3,2},{4,5},{5,4},{6,7},{7,6},{8,9},{9,8},{10,11... | collective-permute-start | bytes 4718600 | tf_op jit(solution)/shard_map/ppermute | solution.py:242
  37.3 20.5 %collective-permute-start.5 = (f32[2,48,32,128]{3,2,1,0:T(8,128)S(1)}, f32[2,48,32,128]{3,2,1,0:T(8,128)}, u32[]{:S(2)}, u32[]{:S(2)}) collective-permute-start(f32[2,48,32,128]{3,2,1,0:T(8,128)S(1)} %collective-permute-done.1.refs_8_), channel_id=1, source_target_pairs={{0,2},{1,7},{2,4},{3,1},{4,6},{5,3},{6,0},{7,5},{8,10},{9,15},{10,... | collective-permute-start | bytes 4718600 | tf_op jit(solution)/shard_map/ppermute | solution.py:242
  38.1 26.3 %collective-permute-start.7 = (f32[2,48,32,128]{3,2,1,0:T(8,128)S(1)}, f32[2,48,32,128]{3,2,1,0:T(8,128)}, u32[]{:S(2)}, u32[]{:S(2)}) collective-permute-start(f32[2,48,32,128]{3,2,1,0:T(8,128)S(1)} %collective-permute-done.1.refs_8_), channel_id=1, source_target_pairs={{2,122},{5,13},{10,2},{13,21},{18,10},{21,29},{26,18},{29,37},{34,... | collective-permute-start | bytes 4718600 | tf_op jit(solution)/shard_map/ppermute | solution.py:242
  46.5 20.4 %collective-permute-start.9 = (f32[2,48,32,128]{3,2,1,0:T(8,128)S(1)}, f32[2,48,32,128]{3,2,1,0:T(8,128)}, u32[]{:S(2)}, u32[]{:S(2)}) collective-permute-start(f32[2,48,32,128]{3,2,1,0:T(8,128)S(1)} %collective-permute-done.2.refs_9_), channel_id=1, source_target_pairs={{1,9},{6,126},{9,17},{14,6},{17,25},{22,14},{25,33},{30,22},{33,41... | collective-permute-start | bytes 4718600 | tf_op jit(solution)/shard_map/ppermute | solution.py:242
  48.3 22.8 %collective-permute-start.3 = (f32[2,48,32,128]{3,2,1,0:T(8,128)S(1)}, f32[2,48,32,128]{3,2,1,0:T(8,128)}, u32[]{:S(2)}, u32[]{:S(2)}) collective-permute-start(f32[2,48,32,128]{3,2,1,0:T(8,128)S(1)} %collective-permute-done.1.refs_8_), channel_id=1, source_target_pairs={{0,1},{1,0},{2,3},{3,2},{4,5},{5,4},{6,7},{7,6},{8,9},{9,8},{10,11... | collective-permute-start | bytes 4718600 | tf_op jit(solution)/shard_map/ppermute | solution.py:242
  48.3 1.1 copy-start.1
  49.5 21.7 %collective-permute-start.4 = (f32[2,48,32,128]{3,2,1,0:T(8,128)S(1)}, f32[2,48,32,128]{3,2,1,0:T(8,128)}, u32[]{:S(2)}, u32[]{:S(2)}) collective-permute-start(f32[2,48,32,128]{3,2,1,0:T(8,128)S(1)} %collective-permute-done.2.refs_9_), channel_id=1, source_target_pairs={{0,1},{1,0},{2,3},{3,2},{4,5},{5,4},{6,7},{7,6},{8,9},{9,8},{10,11... | collective-permute-start | bytes 4718600 | tf_op jit(solution)/shard_map/ppermute | solution.py:242
  57.8 33.0 %collective-permute-start.6 = (f32[2,48,32,128]{3,2,1,0:T(8,128)}, f32[2,48,32,128]{3,2,1,0:T(8,128)}, u32[]{:S(2)}, u32[]{:S(2)}) collective-permute-start(f32[2,48,32,128]{3,2,1,0:T(8,128)} %collective-permute-done.5.refs_12_), channel_id=1, source_target_pairs={{0,1},{1,0},{2,3},{3,2},{4,5},{5,4},{6,7},{7,6},{8,9},{9,8},{10,11... | collective-permute-start | bytes 4718600 | tf_op jit(solution)/shard_map/ppermute | solution.py:242
  64.4 26.4 %collective-permute-start.8 = (f32[2,48,32,128]{3,2,1,0:T(8,128)}, f32[2,48,32,128]{3,2,1,0:T(8,128)}, u32[]{:S(2)}, u32[]{:S(2)}) collective-permute-start(f32[2,48,32,128]{3,2,1,0:T(8,128)} %collective-permute-done.7.refs_14_), channel_id=1, source_target_pairs={{2,3},{5,4},{10,11},{13,12},{18,19},{21,20},{26,27},{29,28},{34,35... | collective-permute-start | bytes 4718600 | tf_op jit(solution)/shard_map/ppermute | solution.py:242
  66.9 23.9 %collective-permute-start.10 = (f32[2,48,32,128]{3,2,1,0:T(8,128)}, f32[2,48,32,128]{3,2,1,0:T(8,128)}, u32[]{:S(2)}, u32[]{:S(2)}) collective-permute-start(f32[2,48,32,128]{3,2,1,0:T(8,128)} %collective-permute-done.9.refs_16_), channel_id=1, source_target_pairs={{1,0},{6,7},{9,8},{14,15},{17,16},{22,23},{25,24},{30,31},{33,32},... | collective-permute-start | bytes 4718600 | tf_op jit(solution)/shard_map/ppermute | solution.py:242
  71.2 1.4 %copy-start = (f32[2,48,32,128]{3,2,1,0:T(8,128)S(1)}, f32[2,48,32,128]{3,2,1,0:T(8,128)}, u32[]{:S(2)}) copy-start(f32[2,48,32,128]{3,2,1,0:T(8,128)} %refs_6_.5) | copy-start | bytes 4718596
  72.6 1.4 %copy-start.2 = (f32[2,48,32,128]{3,2,1,0:T(8,128)S(1)}, f32[2,48,32,128]{3,2,1,0:T(8,128)}, u32[]{:S(2)}) copy-start(f32[2,48,32,128]{3,2,1,0:T(8,128)} %copy-done.1) | copy-start | bytes 4718596
  74.0 0.7 copy-start.4
  74.6 0.7 copy-start.5
  75.3 0.7 copy-start.6
  90.8 11.6 %copy-start.3 = (f32[2,48,32,128]{3,2,1,0:T(8,128)S(1)}, f32[2,48,32,128]{3,2,1,0:T(8,128)}, u32[]{:S(2)}) copy-start(f32[2,48,32,128]{3,2,1,0:T(8,128)} %refs_18_.1) | copy-start | bytes 4718596
  96.5 36.5 %collective-permute-start.11 = (f32[2,48,32,128]{3,2,1,0:T(8,128)S(1)}, f32[2,48,32,128]{3,2,1,0:T(8,128)S(1)}, u32[]{:S(2)}, u32[]{:S(2)}) collective-permute-start(f32[2,48,32,128]{3,2,1,0:T(8,128)S(1)} %get-tuple-element.11), channel_id=1, source_target_pairs={{0,120},{1,121},{2,122},{3,123},{4,124},{5,125},{6,126},{7,127},{8... | collective-permute-start | bytes 4718600 | tf_op jit(solution)/shard_map/ppermute | solution.py:242
  102.4 36.1 %copy-start.7 = (f32[2,48,32,128]{3,2,1,0:T(8,128)S(1)}, f32[2,48,32,128]{3,2,1,0:T(8,128)}, u32[]{:S(2)}) copy-start(f32[2,48,32,128]{3,2,1,0:T(8,128)} %param.11) | copy-start | bytes 4718596
  102.4 36.1 %collective-permute-start.12 = (f32[2,48,32,128]{3,2,1,0:T(8,128)S(1)}, f32[2,48,32,128]{3,2,1,0:T(8,128)S(1)}, u32[]{:S(2)}, u32[]{:S(2)}) collective-permute-start(f32[2,48,32,128]{3,2,1,0:T(8,128)S(1)} %get-tuple-element.12), channel_id=1, source_target_pairs={{0,8},{1,9},{2,10},{3,11},{4,12},{5,13},{6,14},{7,15},{8,16},{9,17... | collective-permute-start | bytes 4718600 | tf_op jit(solution)/shard_map/ppermute | solution.py:242

commit v2 on v1

--- a/solution.py
+++ b/solution.py
@@ -2,16 +2,17 @@
 
 import jax
 import jax.numpy as jnp
-import numpy as np
 from jax import lax
 from jax.experimental import pallas as pl
 from jax.experimental.pallas import tpu as pltpu
 from jax.sharding import PartitionSpec as P
 
+
 NCTRL = 16
 ROW = 8
 NX4 = 4
 UNROLL = 16
+VMEM_LIMIT = 60 * 2**20
 
 HBM = pltpu.MemorySpace.HBM
 SMEM = pltpu.MemorySpace.SMEM
@@ -20,34 +21,22 @@
 N_EARLY = 6
 
 
-def source_table():
-    table = np.zeros((ROW, 9), np.int32)
-    for i in range(ROW):
-        x, c = i // 2, i % 2
-        first = -1 if x % 2 == 0 else 0
-        for q in range(9):
-            s = first + q
-            if s < 0 or s >= ROW:
-                if x in (1, 2):
-                    direct = 0 if x == 1 else 1
-                    table[i, q] = HA if c == direct else HXA
-                else:
-                    direct = 0 if x == 3 else 1
-                    table[i, q] = HB if c == direct else HXB
-                continue
-            other = (s % 2) != c
-            delta = (s // 2 - x) % NX4
-            if delta == 0:
-                table[i, q] = SIB if other else OWN
-            elif delta == 2:
-                table[i, q] = XQ if other else Q
-            elif (delta == 1) == (c == 0):
-                table[i, q] = XA if other else PB
-                if delta == 3:
-                    table[i, q] = XA if other else PB
-            else:
-                table[i, q] = XB if other else PA
-    return table
+def source_of(i, s):
+    x, c = jnp.right_shift(i, 1), jnp.bitwise_and(i, 1)
+    other = jnp.bitwise_and(s, 1) != c
+    delta = jnp.bitwise_and(jnp.right_shift(s, 1) - x, NX4 - 1)
+    near = jnp.where(
+        (delta == 1) == (c == 0), jnp.where(other, XA, PB), jnp.where(other, XB, PA)
+    )
+    inside = jnp.where(
+        delta == 0,
+        jnp.where(other, SIB, OWN),
+        jnp.where(delta == 2, jnp.where(other, XQ, Q), near),
+    )
+    middle = jnp.logical_or(x == 1, x == 2)
+    direct = jnp.where(jnp.bitwise_and(x, 1) == 1, 0, 1) == c
+    halo = jnp.where(middle, jnp.where(direct, HA, HXA), jnp.where(direct, HB, HXB))
+    return jnp.where(jnp.logical_or(s < 0, s >= ROW), halo, inside)
 
 
 def pairs(count, rule):
@@ -67,21 +56,24 @@
 
 
 def control_kernel(mode, nsrc, *refs):
-    meta, so, co, goff, frac, cost = refs[:6]
-    src = refs[6:6 + nsrc]
-    refs = refs[6 + nsrc:]
+    so, co, goff, frac, cost = refs[:5]
+    src = refs[5:5 + nsrc]
+    refs = refs[5 + nsrc:]
     nbest = 1 if mode == "rest" else 2
     ninit = {"early": 0, "late": 2, "rest": 1}[mode]
     init, refs = refs[:ninit], refs[ninit:]
     outs, refs = refs[:nbest], refs[nbest:]
-    buf, best, todo, sem, io_sem = refs
+    buf, best, todo, where, sem, io_sem = refs
     ny, nz = best.shape[2], best.shape[3]
 
     inits = [pltpu.make_async_copy(init[b], best.at[b], io_sem.at[b]) for b in range(ninit)]
     for copy in inits:
         copy.start()
 
-    i, first = meta[0], meta[1]
+    i = lax.rem(lax.axis_index("gx"), ROW)
+    first = -jnp.bitwise_and(1 - jnp.right_shift(i, 1), 1)
+    for q in range(9):
+        where[q] = source_of(i, first + q)
 
     def place(u):
         at = i + so[u] - first
@@ -90,7 +82,7 @@
 
     def listed(u, n):
         a, q = place(u)
-        early = jnp.logical_and(meta[2 + q] < N_EARLY, meta[3 + q] < N_EARLY)
+        early = jnp.logical_and(where[q] < N_EARLY, where[q + 1] < N_EARLY)
         if mode == "rest":
             take = a == 0
         elif mode == "early":
@@ -123,7 +115,7 @@
         def _(t):
             at = co[u] + t
             half = jnp.bitwise_and(at, 1)
-            which = meta[2 + q + jnp.right_shift(at, 1)]
+            which = where[q + jnp.right_shift(at, 1)]
             for n in range(nsrc):
 
                 @pl.when(which == n)
@@ -136,9 +128,9 @@
         slot = lax.rem(k, 2)
         a, _ = place(u)
         b = 0 if mode == "rest" else jnp.where(a > 0, 0, 1)
-        f = [frac[4 * u + d] for d in range(4)]
+        f = [frac[u, d] for d in range(4)]
         g = [1.0 - x for x in f]
-        g1, g2, g3 = (goff[3 * u + d] for d in range(3))
+        g1, g2, g3 = (goff[u, d] for d in range(3))
         pay = cost[u]
         low, high = [], []
         for v in range(nz // 8):
@@ -226,12 +218,12 @@
             pltpu.VMEM((2, 3, shape[1], shape[2] + 8, shape[3]), jnp.float32),
             pltpu.VMEM((nbest,) + shape, jnp.float32),
             pltpu.SMEM((NCTRL,), jnp.int32),
+            pltpu.SMEM((9,), jnp.int32),
             pltpu.SemaphoreType.DMA((2,)),
             pltpu.SemaphoreType.DMA((2,)),
         ],
-        compiler_params=pltpu.CompilerParams(vmem_limit_bytes=24 * 2**20),
+        compiler_params=pltpu.CompilerParams(vmem_limit_bytes=VMEM_LIMIT),
         cost_estimate=pl.CostEstimate(flops=flops, bytes_accessed=2**20, transcendentals=0),
-        name="controls_" + mode,
     )(*params, *sources, *init)
 
 
@@ -242,39 +234,29 @@
         return lax.ppermute(x, "gx", pairs(size, rule))
 
     swap = lambda r, x, c: (r, x, 1 - c)
-    chips = lambda members, rule: lambda r, x, c: rule(r, x, c) if x in members else None
-
-    pa = move(value, lambda r, x, c: (r, x + 1 - 2 * c, c))
-    pb = move(value, lambda r, x, c: (r, x - 1 + 2 * c, c))
+    forth = lambda r, x, c: (r, x + 1 - 2 * c, c)
+    back = lambda r, x, c: (r, x - 1 + 2 * c, c)
+    halo = lambda up, down: lambda r, x, c: (
+        (r - 1, x, c) if (x, c) == up else (r + 1, x, c) if (x, c) == down else None
+    )
+    swap_on = lambda *who: lambda r, x, c: (r, x, 1 - c) if (x, c) in who else None
+
+    pa = move(value, forth)
+    pb = move(value, back)
     sib = move(value, swap)
-    q = move(pa, lambda r, x, c: (r, x + 1 - 2 * c, c))
+    q = move(pa, forth)
     xa = move(pa, swap)
     xb = move(pb, swap)
-    halo = lambda up, down: lambda r, x, c: (
-        (r - 1, x, c) if (x, c) == up else (r + 1, x, c) if (x, c) == down else None
-    )
     ha = move(pa, halo((1, 0), (2, 1)))
     hb = move(pb, halo((3, 0), (0, 1)))
-    hxa = move(ha, lambda r, x, c: (r, x, 1 - c) if (x, c) in ((1, 0), (2, 1)) else None)
-    hxb = move(hb, lambda r, x, c: (r, x, 1 - c) if (x, c) in ((3, 0), (0, 1)) else None)
     xq = move(q, swap)
-
-    i = lax.rem(lax.axis_index("gx"), ROW)
-    table = source_table()
-    first = np.array([-1 if (k // 2) % 2 == 0 else 0 for k in range(ROW)], np.int32)
-    meta = jnp.asarray(np.concatenate([np.arange(ROW, dtype=np.int32)[:, None], first[:, None], table], 1))
-    meta = lax.dynamic_index_in_dim(meta, i, 0, keepdims=False)
-    params = (
-        meta,
-        shard_offset,
-        cell_offset,
-        grid_offset.reshape(-1),
-        fractions.reshape(-1),
-        control_cost,
-    )
-    early = [value, sib, pa, pb, xa, xb]
-    full = early + [q, xq, ha, hxa, hb, hxb]
-    up, down = run_controls("early", params, early, [], 2 * 10**7)
+    hxa = move(ha, swap_on((1, 0), (2, 1)))
+    hxb = move(hb, swap_on((3, 0), (0, 1)))
+
+    params = (shard_offset, cell_offset, grid_offset, fractions, control_cost)
+    near = [value, sib, pa, pb, xa, xb]
+    full = near + [q, xq, ha, hxa, hb, hxb]
+    up, down = run_controls("early", params, near, [], 2 * 10**7)
     up, down = run_controls("late", params, full, [up, down], 10**7)
     got_up = move(up, lambda r, x, c: (r - 1, x, c))
     got_down = move(down, lambda r, x, c: (r + 1, x, c))

time: 140 us -> 147 us (1.050)
  the two profiles are of different devices: /device:TPU:2 before, /device:TPU:0 now
where the time goes in v2:
time: 147 us; the launch traced here: 145 us
  waiting for transfers between devices  80.5 us (55%)
  Pallas kernels  37.9 us (26%)
  starting transfers between devices  19.7 us (13%)
  other arithmetic  3.78 us (3%)
  local copies, waits for them, and re-layouts  2.72 us (2%)
    ppermute x13, waiting for transfers between devices, move(): return lax.ppermute(x, 'gx', pairs(size, rule))  80.5 us
    pallas_call x3, Pallas kernels, run_controls(): pl.pallas_call(functools.partial(control_kernel, mode, len(sources)), out...  37.9 us
    ppermute x13, starting transfers between devices, move(): return lax.ppermute(x, 'gx', pairs(size, rule))  19.7 us
    max x1, other arithmetic, body(): jnp.maximum(obstacle, jnp.minimum(mine, jnp.minimum(got_up, got_down)))  3.78 us
  transfers between devices with their start and end apart: 13, of which 4 were waited for; matrix products, arithmetic and copies ran while one was open for 2% of the time, Pallas kernels for 19%

profile of v2, /device:TPU:0, one launch (start us, length us, event | category | flops | bytes accessed | tf_op | source)
XLA Modules:
  0.0 144.7 jit_solution(14604251666820289977)
XLA Ops:
  0.0 1.6 %collective-permute-start.1 = (f32[2,48,32,128]{3,2,1,0:T(8,128)}, f32[2,48,32,128]{3,2,1,0:T(8,128)S(1)}, u32[]{:S(2)}, u32[]{:S(2)}) collective-permute-start(f32[2,48,32,128]{3,2,1,0:T(8,128)} %refs_5_.5), channel_id=1, source_target_pairs={{0,2},{1,7},{2,4},{3,1},{4,6},{5,3},{6,0},{7,5},{8,10},{9,15},{10,... | collective-permute-start | bytes 4718600 | tf_op jit(solution)/shard_map/ppermute | solution.py:234
  1.6 1.6 %collective-permute-start.2 = (f32[2,48,32,128]{3,2,1,0:T(8,128)}, f32[2,48,32,128]{3,2,1,0:T(8,128)S(1)}, u32[]{:S(2)}, u32[]{:S(2)}) collective-permute-start(f32[2,48,32,128]{3,2,1,0:T(8,128)} %refs_5_.5), channel_id=1, source_target_pairs={{0,6},{1,3},{2,0},{3,5},{4,2},{5,7},{6,4},{7,1},{8,14},{9,11},{10,... | collective-permute-start | bytes 4718600 | tf_op jit(solution)/shard_map/ppermute | solution.py:234
  3.2 0.0 collective-permute-start
  3.2 34.0 %collective-permute-done.1.refs_7_ = f32[2,48,32,128]{3,2,1,0:T(8,128)S(1)} collective-permute-done((f32[2,48,32,128]{3,2,1,0:T(8,128)}, f32[2,48,32,128]{3,2,1,0:T(8,128)S(1)}, u32[]{:S(2)}, u32[]{:S(2)}) %collective-permute-start.1) | collective-permute-done | bytes 1572896 | tf_op jit(solution)/shard_map/ppermute | solution.py:234
  37.2 0.0 copy-start
  37.2 1.7 %collective-permute-start.5 = (f32[2,48,32,128]{3,2,1,0:T(8,128)S(1)}, f32[2,48,32,128]{3,2,1,0:T(8,128)}, u32[]{:S(2)}, u32[]{:S(2)}) collective-permute-start(f32[2,48,32,128]{3,2,1,0:T(8,128)S(1)} %collective-permute-done.1.refs_7_), channel_id=1, source_target_pairs={{0,2},{1,7},{2,4},{3,1},{4,6},{5,3},{6,0},{7,5},{8,10},{9,15},{10,... | collective-permute-start | bytes 4718600 | tf_op jit(solution)/shard_map/ppermute | solution.py:234
  38.9 1.8 %collective-permute-start.7 = (f32[2,48,32,128]{3,2,1,0:T(8,128)S(1)}, f32[2,48,32,128]{3,2,1,0:T(8,128)}, u32[]{:S(2)}, u32[]{:S(2)}) collective-permute-start(f32[2,48,32,128]{3,2,1,0:T(8,128)S(1)} %collective-permute-done.1.refs_7_), channel_id=1, source_target_pairs={{2,122},{5,13},{10,2},{13,21},{18,10},{21,29},{26,18},{29,37},{34,... | collective-permute-start | bytes 4718600 | tf_op jit(solution)/shard_map/ppermute | solution.py:234
  40.7 0.0 collective-permute-done.2.refs_8_
  40.7 0.0 copy-start.1
  40.7 1.8 %collective-permute-start.9 = (f32[2,48,32,128]{3,2,1,0:T(8,128)S(1)}, f32[2,48,32,128]{3,2,1,0:T(8,128)}, u32[]{:S(2)}, u32[]{:S(2)}) collective-permute-start(f32[2,48,32,128]{3,2,1,0:T(8,128)S(1)} %collective-permute-done.2.refs_8_), channel_id=1, source_target_pairs={{1,9},{6,126},{9,17},{14,6},{17,25},{22,14},{25,33},{30,22},{33,41... | collective-permute-start | bytes 4718600 | tf_op jit(solution)/shard_map/ppermute | solution.py:234
  42.6 1.2 collective-permute-start.3
  43.7 0.0 collective-permute-done.refs_6_
  43.7 0.0 copy-start.2
  43.7 0.1 collective-permute-start.4
  43.9 15.1 %collective-permute-done.5.refs_11_ = f32[2,48,32,128]{3,2,1,0:T(8,128)} collective-permute-done((f32[2,48,32,128]{3,2,1,0:T(8,128)S(1)}, f32[2,48,32,128]{3,2,1,0:T(8,128)}, u32[]{:S(2)}, u32[]{:S(2)}) %collective-permute-start.5) | collective-permute-done | bytes 1572896 | tf_op jit(solution)/shard_map/ppermute | solution.py:234
  59.0 0.0 collective-permute-start.6
  59.0 0.0 collective-permute-done.7.refs_13_
  59.0 1.8 %collective-permute-start.8 = (f32[2,48,32,128]{3,2,1,0:T(8,128)}, f32[2,48,32,128]{3,2,1,0:T(8,128)}, u32[]{:S(2)}, u32[]{:S(2)}) collective-permute-start(f32[2,48,32,128]{3,2,1,0:T(8,128)} %collective-permute-done.7.refs_13_), channel_id=1, source_target_pairs={{2,3},{5,4},{10,11},{13,12},{18,19},{21,20},{26,27},{29,28},{34,35... | collective-permute-start | bytes 4718600 | tf_op jit(solution)/shard_map/ppermute | solution.py:234
  60.8 0.0 collective-permute-done.9.refs_15_
  60.8 0.0 copy-done.2
  60.8 1.3 collective-permute-start.10
  62.1 1.4 copy.10.refs_3_
  63.4 1.4 copy.9.refs_2_
  64.8 0.0 collective-permute-done.3.refs_9_
  64.8 0.0 collective-permute-done.4.refs_10_
  64.8 0.0 copy-done
  64.8 0.0 copy-done.1
  64.8 18.4 %shard_map.83 = (f32[2,48,32,128]{3,2,1,0:T(8,128)}, f32[2,48,32,128]{3,2,1,0:T(8,128)}) custom-call(s32[16]{0:T(128)} %refs_0_.5, s32[16]{0:T(128)} %refs_1_.5, s32[16,3]{1,0:T(8,128)} %copy.9.refs_2_, f32[16,4]{1,0:T(8,128)} %copy.10.refs_3_, f32[16]{0:T(128)} %refs_4_.5, f32[2,48,32,128]{3,2,1,0:T(8,128)} %refs_5_.5, f32[2,48,32,128]{3,2,1,0:T(8,128)} %copy-done.2, ...), custom_call_target="tpu_custom_call" | custom-call | flops 20000000 | bytes 1048576 | tf_op jit(solution)/shard_map/pallas_call | solution.py:211
  83.2 0.0 collective-permute-done.6.refs_12_
  83.2 0.0 collective-permute-done.8.refs_14_
  83.2 0.0 collective-permute-done.10.refs_16_
  83.2 10.9 %shard_map.84 = (f32[2,48,32,128]{3,2,1,0:T(8,128)}, f32[2,48,32,128]{3,2,1,0:T(8,128)}) custom-call(s32[16]{0:T(128)} %refs_0_.5, s32[16]{0:T(128)} %refs_1_.5, s32[16,3]{1,0:T(8,128)} %copy.9.refs_2_, f32[16,4]{1,0:T(8,128)} %copy.10.refs_3_, f32[16]{0:T(128)} %refs_4_.5, f32[2,48,32,128]{3,2,1,0:T(8,128)} %refs_5_.5, f32[2,48,32,128]{3,2,1,0:T(8,128)} %copy-done.2, ...), custom_call_target="tpu_custom_call" | custom-call | flops 10000000 | bytes 1048576 | tf_op jit(solution)/shard_map/pallas_call | solution.py:211
  94.2 6.8 %collective-permute-start.11 = (f32[2,48,32,128]{3,2,1,0:T(8,128)}, f32[2,48,32,128]{3,2,1,0:T(8,128)S(1)}, u32[]{:S(2)}, u32[]{:S(2)}) collective-permute-start(f32[2,48,32,128]{3,2,1,0:T(8,128)} %get-tuple-element.11), channel_id=1, source_target_pairs={{0,120},{1,121},{2,122},{3,123},{4,124},{5,125},{6,126},{7,127},{8... | collective-permute-start | bytes 4718600 | tf_op jit(solution)/shard_map/ppermute | solution.py:234
  101.0 0.0 copy-start.3
  101.0 0.0 collective-permute-start.12
  101.0 8.6 %shard_map.82 = f32[2,48,32,128]{3,2,1,0:T(8,128)} custom-call(s32[16]{0:T(128)} %refs_0_.5, s32[16]{0:T(128)} %refs_1_.5, s32[16,3]{1,0:T(8,128)} %copy.9.refs_2_, f32[16,4]{1,0:T(8,128)} %copy.10.refs_3_, f32[16]{0:T(128)} %refs_4_.5, f32[2,48,32,128]{3,2,1,0:T(8,128)} %refs_5_.5, f32[2,48,32,128]{3,2,1,0:T(8,128)} %copy-done.2, ...), custom_call_target="tpu_custom_call" | custom-call | flops 30000000 | bytes 1048576 | tf_op jit(solution)/shard_map/pallas_call | solution.py:211
  109.6 25.3 %collective-permute-done.11 = f32[2,48,32,128]{3,2,1,0:T(8,128)S(1)} collective-permute-done((f32[2,48,32,128]{3,2,1,0:T(8,128)}, f32[2,48,32,128]{3,2,1,0:T(8,128)S(1)}, u32[]{:S(2)}, u32[]{:S(2)}) %collective-permute-start.11) | collective-permute-done | bytes 1572896 | tf_op jit(solution)/shard_map/ppermute | solution.py:234
  134.9 6.1 %collective-permute-done.12 = f32[2,48,32,128]{3,2,1,0:T(8,128)} collective-permute-done((f32[2,48,32,128]{3,2,1,0:T(8,128)}, f32[2,48,32,128]{3,2,1,0:T(8,128)}, u32[]{:S(2)}, u32[]{:S(2)}) %collective-permute-start.12) | collective-permute-done | bytes 1572896 | tf_op jit(solution)/shard_map/ppermute | solution.py:234
  140.9 0.0 copy-done.3
  140.9 3.8 %minimum_maximum_fusion = f32[2,48,32,128]{3,2,1,0:T(8,128)} fusion(f32[2,48,32,128]{3,2,1,0:T(8,128)S(1)} %copy-done.3, f32[2,48,32,128]{3,2,1,0:T(8,128)} %shard_map.82, f32[2,48,32,128]{3,2,1,0:T(8,128)S(1)} %collective-permute-done.11, f32[2,48,32,128]{3,2,1,0:T(8,128)} %collective-permute-done.12), kind=kLoop, calls=%fused_computation | loop fusion | flops 1179648 | bytes 7864320 | tf_op jit(solution)/shard_map/max | solution.py:264
Async XLA Ops:
  0.0 37.2 %collective-permute-start.1 = (f32[2,48,32,128]{3,2,1,0:T(8,128)}, f32[2,48,32,128]{3,2,1,0:T(8,128)S(1)}, u32[]{:S(2)}, u32[]{:S(2)}) collective-permute-start(f32[2,48,32,128]{3,2,1,0:T(8,128)} %refs_5_.5), channel_id=1, source_target_pairs={{0,2},{1,7},{2,4},{3,1},{4,6},{5,3},{6,0},{7,5},{8,10},{9,15},{10,... | collective-permute-start | bytes 4718600 | tf_op jit(solution)/shard_map/ppermute | solution.py:234
  1.6 39.1 %collective-permute-start.2 = (f32[2,48,32,128]{3,2,1,0:T(8,128)}, f32[2,48,32,128]{3,2,1,0:T(8,128)S(1)}, u32[]{:S(2)}, u32[]{:S(2)}) collective-permute-start(f32[2,48,32,128]{3,2,1,0:T(8,128)} %refs_5_.5), channel_id=1, source_target_pairs={{0,6},{1,3},{2,0},{3,5},{4,2},{5,7},{6,4},{7,1},{8,14},{9,11},{10,... | collective-permute-start | bytes 4718600 | tf_op jit(solution)/shard_map/ppermute | solution.py:234
  3.2 40.5 %collective-permute-start = (f32[2,48,32,128]{3,2,1,0:T(8,128)}, f32[2,48,32,128]{3,2,1,0:T(8,128)S(1)}, u32[]{:S(2)}, u32[]{:S(2)}) collective-permute-start(f32[2,48,32,128]{3,2,1,0:T(8,128)} %refs_5_.5), channel_id=1, source_target_pairs={{0,1},{1,0},{2,3},{3,2},{4,5},{5,4},{6,7},{7,6},{8,9},{9,8},{10,11... | collective-permute-start | bytes 4718600 | tf_op jit(solution)/shard_map/ppermute | solution.py:234
  37.2 27.6 %copy-start = (f32[2,48,32,128]{3,2,1,0:T(8,128)}, f32[2,48,32,128]{3,2,1,0:T(8,128)S(1)}, u32[]{:S(2)}) copy-start(f32[2,48,32,128]{3,2,1,0:T(8,128)S(1)} %collective-permute-done.1.refs_7_) | copy-start | bytes 4718596
  37.2 21.7 %collective-permute-start.5 = (f32[2,48,32,128]{3,2,1,0:T(8,128)S(1)}, f32[2,48,32,128]{3,2,1,0:T(8,128)}, u32[]{:S(2)}, u32[]{:S(2)}) collective-permute-start(f32[2,48,32,128]{3,2,1,0:T(8,128)S(1)} %collective-permute-done.1.refs_7_), channel_id=1, source_target_pairs={{0,2},{1,7},{2,4},{3,1},{4,6},{5,3},{6,0},{7,5},{8,10},{9,15},{10,... | collective-permute-start | bytes 4718600 | tf_op jit(solution)/shard_map/ppermute | solution.py:234
  38.9 20.1 %collective-permute-start.7 = (f32[2,48,32,128]{3,2,1,0:T(8,128)S(1)}, f32[2,48,32,128]{3,2,1,0:T(8,128)}, u32[]{:S(2)}, u32[]{:S(2)}) collective-permute-start(f32[2,48,32,128]{3,2,1,0:T(8,128)S(1)} %collective-permute-done.1.refs_7_), channel_id=1, source_target_pairs={{2,122},{5,13},{10,2},{13,21},{18,10},{21,29},{26,18},{29,37},{34,... | collective-permute-start | bytes 4718600 | tf_op jit(solution)/shard_map/ppermute | solution.py:234
  40.7 24.1 %copy-start.1 = (f32[2,48,32,128]{3,2,1,0:T(8,128)}, f32[2,48,32,128]{3,2,1,0:T(8,128)S(1)}, u32[]{:S(2)}) copy-start(f32[2,48,32,128]{3,2,1,0:T(8,128)S(1)} %collective-permute-done.2.refs_8_) | copy-start | bytes 4718596
  40.7 20.1 %collective-permute-start.9 = (f32[2,48,32,128]{3,2,1,0:T(8,128)S(1)}, f32[2,48,32,128]{3,2,1,0:T(8,128)}, u32[]{:S(2)}, u32[]{:S(2)}) collective-permute-start(f32[2,48,32,128]{3,2,1,0:T(8,128)S(1)} %collective-permute-done.2.refs_8_), channel_id=1, source_target_pairs={{1,9},{6,126},{9,17},{14,6},{17,25},{22,14},{25,33},{30,22},{33,41... | collective-permute-start | bytes 4718600 | tf_op jit(solution)/shard_map/ppermute | solution.py:234
  42.6 22.2 %collective-permute-start.3 = (f32[2,48,32,128]{3,2,1,0:T(8,128)S(1)}, f32[2,48,32,128]{3,2,1,0:T(8,128)}, u32[]{:S(2)}, u32[]{:S(2)}) collective-permute-start(f32[2,48,32,128]{3,2,1,0:T(8,128)S(1)} %collective-permute-done.1.refs_7_), channel_id=1, source_target_pairs={{0,1},{1,0},{2,3},{3,2},{4,5},{5,4},{6,7},{7,6},{8,9},{9,8},{10,11... | collective-permute-start | bytes 4718600 | tf_op jit(solution)/shard_map/ppermute | solution.py:234
  43.7 17.1 %copy-start.2 = (f32[2,48,32,128]{3,2,1,0:T(8,128)}, f32[2,48,32,128]{3,2,1,0:T(8,128)S(1)}, u32[]{:S(2)}) copy-start(f32[2,48,32,128]{3,2,1,0:T(8,128)S(1)} %collective-permute-done.refs_6_) | copy-start | bytes 4718596
  43.7 21.1 %collective-permute-start.4 = (f32[2,48,32,128]{3,2,1,0:T(8,128)S(1)}, f32[2,48,32,128]{3,2,1,0:T(8,128)}, u32[]{:S(2)}, u32[]{:S(2)}) collective-permute-start(f32[2,48,32,128]{3,2,1,0:T(8,128)S(1)} %collective-permute-done.2.refs_8_), channel_id=1, source_target_pairs={{0,1},{1,0},{2,3},{3,2},{4,5},{5,4},{6,7},{7,6},{8,9},{9,8},{10,11... | collective-permute-start | bytes 4718600 | tf_op jit(solution)/shard_map/ppermute | solution.py:234
  59.0 24.3 %collective-permute-start.6 = (f32[2,48,32,128]{3,2,1,0:T(8,128)}, f32[2,48,32,128]{3,2,1,0:T(8,128)}, u32[]{:S(2)}, u32[]{:S(2)}) collective-permute-start(f32[2,48,32,128]{3,2,1,0:T(8,128)} %collective-permute-done.5.refs_11_), channel_id=1, source_target_pairs={{0,1},{1,0},{2,3},{3,2},{4,5},{5,4},{6,7},{7,6},{8,9},{9,8},{10,11... | collective-permute-start | bytes 4718600 | tf_op jit(solution)/shard_map/ppermute | solution.py:234
  59.0 24.3 %collective-permute-start.8 = (f32[2,48,32,128]{3,2,1,0:T(8,128)}, f32[2,48,32,128]{3,2,1,0:T(8,128)}, u32[]{:S(2)}, u32[]{:S(2)}) collective-permute-start(f32[2,48,32,128]{3,2,1,0:T(8,128)} %collective-permute-done.7.refs_13_), channel_id=1, source_target_pairs={{2,3},{5,4},{10,11},{13,12},{18,19},{21,20},{26,27},{29,28},{34,35... | collective-permute-start | bytes 4718600 | tf_op jit(solution)/shard_map/ppermute | solution.py:234
  60.8 22.4 %collective-permute-start.10 = (f32[2,48,32,128]{3,2,1,0:T(8,128)}, f32[2,48,32,128]{3,2,1,0:T(8,128)}, u32[]{:S(2)}, u32[]{:S(2)}) collective-permute-start(f32[2,48,32,128]{3,2,1,0:T(8,128)} %collective-permute-done.9.refs_15_), channel_id=1, source_target_pairs={{1,0},{6,7},{9,8},{14,15},{17,16},{22,23},{25,24},{30,31},{33,32},... | collective-permute-start | bytes 4718600 | tf_op jit(solution)/shard_map/ppermute | solution.py:234
  94.2 40.7 %collective-permute-start.11 = (f32[2,48,32,128]{3,2,1,0:T(8,128)}, f32[2,48,32,128]{3,2,1,0:T(8,128)S(1)}, u32[]{:S(2)}, u32[]{:S(2)}) collective-permute-start(f32[2,48,32,128]{3,2,1,0:T(8,128)} %get-tuple-element.11), channel_id=1, source_target_pairs={{0,120},{1,121},{2,122},{3,123},{4,124},{5,125},{6,126},{7,127},{8... | collective-permute-start | bytes 4718600 | tf_op jit(solution)/shard_map/ppermute | solution.py:234
  101.0 40.0 %copy-start.3 = (f32[2,48,32,128]{3,2,1,0:T(8,128)S(1)}, f32[2,48,32,128]{3,2,1,0:T(8,128)}, u32[]{:S(2)}) copy-start(f32[2,48,32,128]{3,2,1,0:T(8,128)} %param.10) | copy-start | bytes 4718596
  101.0 40.0 %collective-permute-start.12 = (f32[2,48,32,128]{3,2,1,0:T(8,128)}, f32[2,48,32,128]{3,2,1,0:T(8,128)}, u32[]{:S(2)}, u32[]{:S(2)}) collective-permute-start(f32[2,48,32,128]{3,2,1,0:T(8,128)} %get-tuple-element.12), channel_id=1, source_target_pairs={{0,8},{1,9},{2,10},{3,11},{4,12},{5,13},{6,14},{7,15},{8,16},{9,17... | collective-permute-start | bytes 4718600 | tf_op jit(solution)/shard_map/ppermute | solution.py:234
